TPU v7x, 32 devices: a whole 2x2x4 slice. The times are simulated.
32 devices in a mesh: rep: 8 (over z, core), tp: 4 (over y, x).
Axes of the slice: x: 2, y: 2, z: 4, core: 2. Of those that a mesh axis runs over, the one named last changes fastest.
Arguments:
- delta_query: bfloat16 [8, 2, 2048, 3072], P('rep', None, None, 'tp'), may hold values from -6 to 6
- master_query: float32 [2, 2048, 3072], P(None, 'rep', 'tp'), may hold values from -3 to 3
- moment_query: float32 [2, 2048, 3072], P(None, 'rep', 'tp'), may hold values from -3 to 3
- delta_latent: bfloat16 [8, 2, 512, 4096], P('rep', None, None, 'tp'), may hold values from -6 to 6
- master_latent: float32 [2, 512, 4096], P(None, 'rep', 'tp'), may hold values from -3 to 3
- moment_latent: float32 [2, 512, 4096], P(None, 'rep', 'tp'), may hold values from -3 to 3
- delta_output: bfloat16 [8, 2, 2048, 2048], P('rep', None, 'tp'), may hold values from -6 to 6
- master_output: float32 [2, 2048, 2048], P(None, 'tp', 'rep'), may hold values from -3 to 3
- moment_output: float32 [2, 2048, 2048], P(None, 'tp', 'rep'), may hold values from -3 to 3
Outputs:
- params_query: bfloat16 [2, 2048, 3072], P(None, None, 'tp')
- new_master_query: float32 [2, 2048, 3072], P(None, 'rep', 'tp')
- new_moment_query: float32 [2, 2048, 3072], P(None, 'rep', 'tp')
- params_latent: bfloat16 [2, 512, 4096], P(None, None, 'tp')
- new_master_latent: float32 [2, 512, 4096], P(None, 'rep', 'tp')
- new_moment_latent: float32 [2, 512, 4096], P(None, 'rep', 'tp')
- params_output: bfloat16 [2, 2048, 2048], P(None, 'tp')
- new_master_output: float32 [2, 2048, 2048], P(None, 'tp', 'rep')
- new_moment_output: float32 [2, 2048, 2048], P(None, 'tp', 'rep')
All inputs are finite; a program needn't handle non-finite values.
Results may differ from a plain program's by a relative error of at most 0.012.
Values may be sent and summed in bfloat16 or wider, within the bound.
A program may use at most 128 MiB of HBM per device.

v0:
```python
import jax
import jax.numpy as jnp
from jax import lax
from jax.sharding import PartitionSpec as P

OUTER_RATE = 0.7
OUTER_MOMENTUM = 0.9


def nesterov(totals, master, moment, replica_count):
    average = totals / replica_count
    momentum = OUTER_MOMENTUM * moment + average
    updated = master - OUTER_RATE * (average + OUTER_MOMENTUM * momentum)
    return (updated, momentum)


def outer_step(
    delta_query,
    master_query,
    moment_query,
    delta_latent,
    master_latent,
    moment_latent,
    delta_output,
    master_output,
    moment_output,
):
    replica_count = lax.axis_size("rep")
    query_totals = lax.psum_scatter(
        delta_query[0].astype(jnp.float32).astype(jnp.bfloat16),
        "rep",
        scatter_dimension=1,
        tiled=True,
    ).astype(jnp.float32)
    latent_totals = lax.psum_scatter(
        delta_latent[0].astype(jnp.float32).astype(jnp.bfloat16),
        "rep",
        scatter_dimension=1,
        tiled=True,
    ).astype(jnp.float32)
    output_totals = lax.psum_scatter(
        delta_output[0].astype(jnp.float32).astype(jnp.bfloat16),
        "rep",
        scatter_dimension=2,
        tiled=True,
    ).astype(jnp.float32)
    query_master, query_moment = nesterov(query_totals, master_query, moment_query, replica_count)
    latent_master, latent_moment = nesterov(
        latent_totals, master_latent, moment_latent, replica_count
    )
    output_master, output_moment = nesterov(
        output_totals, master_output, moment_output, replica_count
    )
    query_params = lax.all_gather(query_master.astype(jnp.bfloat16), "rep", axis=1, tiled=True)
    latent_params = lax.all_gather(latent_master.astype(jnp.bfloat16), "rep", axis=1, tiled=True)
    output_params = lax.all_gather(output_master.astype(jnp.bfloat16), "rep", axis=2, tiled=True)
    return (
        query_params,
        query_master,
        query_moment,
        latent_params,
        latent_master,
        latent_moment,
        output_params,
        output_master,
        output_moment,
    )


def on_device(
    delta_query,
    master_query,
    moment_query,
    delta_latent,
    master_latent,
    moment_latent,
    delta_output,
    master_output,
    moment_output,
):
    return outer_step(
        delta_query,
        master_query,
        moment_query,
        delta_latent,
        master_latent,
        moment_latent,
        delta_output,
        master_output,
        moment_output,
    )


def solution(mesh):
    placed = (
        P("rep", None, None, "tp"),
        P(None, "rep", "tp"),
        P(None, "rep", "tp"),
        P("rep", None, None, "tp"),
        P(None, "rep", "tp"),
        P(None, "rep", "tp"),
        P("rep", None, "tp", None),
        P(None, "tp", "rep"),
        P(None, "tp", "rep"),
    )
    return jax.shard_map(
        on_device,
        mesh=mesh,
        in_specs=placed,
        out_specs=(
            P(None, None, "tp"),
            P(None, "rep", "tp"),
            P(None, "rep", "tp"),
            P(None, None, "tp"),
            P(None, "rep", "tp"),
            P(None, "rep", "tp"),
            P(None, "tp", None),
            P(None, "tp", "rep"),
            P(None, "tp", "rep"),
        ),
        check_vma=False,
    )
```

profile of v0, /device:TPU:0, one launch (start us, length us, event | category | flops | bytes accessed | tf_op | source)
XLA Modules:
  0.0 332.2 jit_solution(7297838098868273898)
XLA Ops:
  7.2 0.0 reduce-scatter.6.cloned.1.call-start
  7.2 0.7 reduce-scatter.6.cloned.1.call-update
  7.9 0.0 reduce-scatter.8.cloned.1.call-start
  8.0 0.7 reduce-scatter.8.cloned.1.call-update
  8.7 0.0 reduce-scatter.4.cloned.1.call-start
  8.7 0.0 copy-start.4
  8.7 0.0 copy-start.5
  8.7 0.7 reduce-scatter.4.cloned.1.call-update
  9.4 0.0 all-gather.6.cloned.1.call-start
  9.4 39.6 %reduce-scatter.6.cloned.1.call-done = bf16[2,64,1024]{2,1,0:T(8,128)(2,1)} async-done(((bf16[2,512,1024]{2,1,0:T(8,128)(2,1)}), bf16[2,64,1024]{2,1,0:T(8,128)(2,1)}) %reduce-scatter.6.cloned.1.call-update) | async-done | bytes 262160 | tf_op jit(solution)/shard_map/reduce_scatter | solution.py:35
  49.1 0.0 copy-done.4
  49.1 0.0 copy-done.5
  49.1 2.1 fusion.1
  51.2 0.0 all-gather.6.cloned.1.call-update
  51.2 0.0 all-gather.8.cloned.1.call-start
  51.3 48.6 %reduce-scatter.8.cloned.1.call-done = bf16[2,512,256]{2,1,0:T(8,128)(2,1)} async-done(((bf16[2,512,2048]{2,1,0:T(8,128)(2,1)}), bf16[2,512,256]{2,1,0:T(8,128)(2,1)}) %reduce-scatter.8.cloned.1.call-update) | async-done | bytes 524304 | tf_op jit(solution)/shard_map/reduce_scatter | solution.py:41
  99.9 0.0 copy-start.2
  99.9 0.0 copy-start.3
  99.9 3.6 %fusion = (bf16[2,512,256]{2,1,0:T(8,128)(2,1)}, f32[2,512,256]{2,1,0:T(8,128)}, f32[2,512,256]{2,1,0:T(8,128)}) fusion(f32[2,512,256]{2,1,0:T(8,128)} %param.16, bf16[2,512,256]{2,1,0:T(8,128)(2,1)} %reduce-scatter.8.cloned.1.call-done, f32[2,512,256]{2,1,0:T(8,128)} %param.17), kind=kLoop, calls=%fused_computation.9 | loop fusion | flops 2359296 | bytes 5242880 | tf_op jit(solution)/shard_map/convert_element_type | solution.py:56
  103.5 0.0 all-gather.8.cloned.1.call-update
  103.6 0.0 all-gather.4.cloned.1.call-start
  103.6 66.8 %reduce-scatter.4.cloned.1.call-done = bf16[2,256,768]{2,1,0:T(8,128)(2,1)} async-done(((bf16[2,2048,768]{2,1,0:T(8,128)(2,1)}), bf16[2,256,768]{2,1,0:T(8,128)(2,1)}) %reduce-scatter.4.cloned.1.call-update) | async-done | bytes 786448 | tf_op jit(solution)/shard_map/reduce_scatter | solution.py:29
  170.4 0.0 copy-done.2
  170.4 0.0 copy-done.3
  170.4 3.5 %fusion.2 = (bf16[2,256,768]{2,1,0:T(8,128)(2,1)}, f32[2,256,768]{2,1,0:T(8,128)}, f32[2,256,768]{2,1,0:T(8,128)}) fusion(f32[2,256,768]{2,1,0:T(8,128)S(1)} %copy-done.2, bf16[2,256,768]{2,1,0:T(8,128)(2,1)} %reduce-scatter.4.cloned.1.call-done, f32[2,256,768]{2,1,0:T(8,128)S(1)} %copy-done.3), kind=kLoop, calls=%fused_computation.11 | loop fusion | flops 3538944 | bytes 7864320 | tf_op jit(solution)/shard_map/convert_element_type | solution.py:54
  173.9 0.0 all-gather.4.cloned.1.call-update
  174.0 26.2 %all-gather.6.cloned.1.call-done = bf16[2,512,1024]{2,1,0:T(8,128)(2,1)} async-done(((bf16[2,64,1024]{2,1,0:T(8,128)(2,1)}), bf16[2,512,1024]{2,1,0:T(8,128)(2,1)}) %all-gather.6.cloned.1.call-update) | async-done | bytes 2097168 | tf_op jit(solution)/shard_map/all_gather | solution.py:55
  200.1 49.3 %all-gather.8.cloned.1.call-done = bf16[2,512,2048]{2,1,0:T(8,128)(2,1)} async-done(((bf16[2,512,256]{2,1,0:T(8,128)(2,1)}), bf16[2,512,2048]{2,1,0:T(8,128)(2,1)}) %all-gather.8.cloned.1.call-update) | async-done | bytes 4194320 | tf_op jit(solution)/shard_map/all_gather | solution.py:56
  249.4 64.9 %all-gather.4.cloned.1.call-done = bf16[2,2048,768]{2,1,0:T(8,128)(2,1)} async-done(((bf16[2,256,768]{2,1,0:T(8,128)(2,1)}), bf16[2,2048,768]{2,1,0:T(8,128)(2,1)}) %all-gather.4.cloned.1.call-update) | async-done | bytes 6291472 | tf_op jit(solution)/shard_map/all_gather | solution.py:54
  314.3 0.0 copy-start.1
  314.3 6.0 %copy.21 = bf16[2,2048,768]{2,1,0:T(8,128)(2,1)} copy(bf16[2,2048,768]{2,1,0:T(8,128)(2,1)} %all-gather.4.cloned.1.call-done) | data formatting | bytes 12582912
  320.4 0.0 copy-done.1
  320.4 0.0 copy-start
  320.4 1.3 copy.22
  321.7 1.6 copy-done
  323.3 2.0 copy.23
Async XLA Ops:
  7.2 41.9 %reduce-scatter.6.cloned.1.call-start = ((), (), s32[]{:S(2)}) async-start(), calls=%async_computation.5 | async-start | bytes 2359296 | tf_op jit(solution)/shard_map/reduce_scatter | solution.py:35
  7.9 92.0 %reduce-scatter.8.cloned.1.call-start = ((), (), s32[]{:S(2)}) async-start(), calls=%async_computation.7 | async-start | bytes 4718592 | tf_op jit(solution)/shard_map/reduce_scatter | solution.py:41
  8.7 161.8 %reduce-scatter.4.cloned.1.call-start = ((), (), s32[]{:S(2)}) async-start(), calls=%async_computation.3 | async-start | bytes 7077888 | tf_op jit(solution)/shard_map/reduce_scatter | solution.py:29
  8.7 40.4 %copy-start.4 = (f32[2,64,1024]{2,1,0:T(8,128)S(1)}, f32[2,64,1024]{2,1,0:T(8,128)}, u32[]{:S(2)}) copy-start(f32[2,64,1024]{2,1,0:T(8,128)} %param.13) | copy-start | bytes 1572868
  8.7 40.3 %copy-start.5 = (f32[2,64,1024]{2,1,0:T(8,128)S(1)}, f32[2,64,1024]{2,1,0:T(8,128)}, u32[]{:S(2)}) copy-start(f32[2,64,1024]{2,1,0:T(8,128)} %param.14) | copy-start | bytes 1572868
  9.4 190.7 %all-gather.6.cloned.1.call-start = ((), (), s32[]{:S(2)}) async-start(), calls=%async_computation.6 | async-start | bytes 2359296 | tf_op jit(solution)/shard_map/all_gather | solution.py:55
  51.2 198.2 %all-gather.8.cloned.1.call-start = ((), (), s32[]{:S(2)}) async-start(), calls=%async_computation.8 | async-start | bytes 4718592 | tf_op jit(solution)/shard_map/all_gather | solution.py:56
  99.9 70.5 %copy-start.2 = (f32[2,256,768]{2,1,0:T(8,128)S(1)}, f32[2,256,768]{2,1,0:T(8,128)}, u32[]{:S(2)}) copy-start(f32[2,256,768]{2,1,0:T(8,128)} %param.10) | copy-start | bytes 4718596
  99.9 70.5 %copy-start.3 = (f32[2,256,768]{2,1,0:T(8,128)S(1)}, f32[2,256,768]{2,1,0:T(8,128)}, u32[]{:S(2)}) copy-start(f32[2,256,768]{2,1,0:T(8,128)} %param.11) | copy-start | bytes 4718596
  103.6 210.8 %all-gather.4.cloned.1.call-start = ((), (), s32[]{:S(2)}) async-start(), calls=%async_computation.4 | async-start | bytes 7077888 | tf_op jit(solution)/shard_map/all_gather | solution.py:54
  314.3 6.0 %copy-start.1 = (bf16[2,512,1024]{2,1,0:T(8,128)(2,1)S(1)}, bf16[2,512,1024]{2,1,0:T(8,128)(2,1)}, u32[]{:S(2)}) copy-start(bf16[2,512,1024]{2,1,0:T(8,128)(2,1)} %all-gather.6.cloned.1.call-done) | copy-start | bytes 6291460
  320.4 2.9 copy-start
Sparse Core Ops, SparseCore 0:
  10.3 38.7 reduce-scatter.5
  51.3 48.5 reduce-scatter.7
  102.2 68.1 reduce-scatter.3
  172.5 27.6 all-gather.5
  202.1 47.1 all-gather.7
  251.4 62.8 all-gather.3
where the time goes:
time: 332 us
  waiting for transfers between devices  298 us (90%)
  between operations  14.1 us (4%)
  local copies, waits for them, and re-layouts  11 us (3%)
  other arithmetic  9.27 us (3%)
    reduce_scatter x1, waiting for transfers between devices, outer_step(): lax.psum_scatter(delta_query[0].astype(jnp.float32).astype(jnp.bfloat16),...  66.8 us
    all_gather x1, waiting for transfers between devices, outer_step(): lax.all_gather(query_master.astype(jnp.bfloat16), 'rep', axis=1, tiled=True)  64.9 us
    all_gather x1, waiting for transfers between devices, outer_step(): lax.all_gather(output_master.astype(jnp.bfloat16), 'rep', axis=2, tiled=T...  49.3 us
    reduce_scatter x1, waiting for transfers between devices, outer_step(): lax.psum_scatter(delta_output[0].astype(jnp.float32).astype(jnp.bfloat16)...  48.6 us
    reduce_scatter x1, waiting for transfers between devices, outer_step(): lax.psum_scatter(delta_latent[0].astype(jnp.float32).astype(jnp.bfloat16)...  39.6 us
    all_gather x1, waiting for transfers between devices, outer_step(): lax.all_gather(latent_master.astype(jnp.bfloat16), 'rep', axis=1, tiled=T...  26.2 us
    unnamed x15, local copies, waits for them, and re-layouts  11 us
  transfers between devices with their start and end apart: 6, of which 6 were waited for; matrix products, arithmetic and copies ran while one was open for 3% of the time, Pallas kernels for 0%

commit v1 on v0

v1 whole, which is shorter than its diff:
```python
import functools

import jax
import jax.numpy as jnp
from jax import lax
from jax.experimental import pallas as pl
from jax.experimental.pallas import tpu as pltpu
from jax.sharding import PartitionSpec as P

OUTER_RATE = 0.7
OUTER_MOMENTUM = 0.9
MESH = pl.DeviceIdType.MESH
PIECES = 16
LEAD = 3


def plan(shapes, pieces):
    cuts = []
    for layers, rows, cols in shapes:
        if pieces % layers:
            return None
        per_layer = pieces // layers
        by_row = per_layer
        while by_row > 1 and (rows % by_row or (rows // by_row) % 16):
            by_row //= 2
        by_col = per_layer // by_row
        if by_row * by_col != per_layer or cols % by_col or (cols // by_col) % 128:
            return None
        cuts.append((per_layer, by_col, rows // by_row, cols // by_col))
    return cuts


def kernel(n, cuts, width, own_shapes, *refs):
    deltas, masters, moments = refs[0:9:3], refs[1:9:3], refs[2:9:3]
    params, new_masters, new_moments = refs[9:18:3], refs[10:18:3], refs[11:18:3]
    (theirs, mine, up_in, down_in, gathered, master, moment) = refs[18:25]
    (theirs_sem, mine_sem, up_sem, down_sem, gather_sem, state_sem,
     gather_up_sem, gather_down_sem, total_sem) = refs[25:]
    m = n // 2
    pieces = theirs.shape[0]
    me = lax.axis_index("rep")
    z, core = me // 2, me % 2
    partner = z * 2 + 1 - core
    above, below = (z + 1) * 2 + core, (z - 1) * 2 + core
    first, last = z == 0, z == m - 1

    def blocks(k):
        found, at = [], 0
        for a, (per_layer, by_col, rows, cols) in enumerate(cuts):
            layer, part = k // per_layer, k % per_layer
            row, col = (part // by_col) * rows, (part % by_col) * cols
            for b in range(cols // width):
                found.append((a, layer, row, rows, col + b * width, at))
                at += rows
        return found

    def whole_slice(a, layer, row, rows, col, owner):
        own_rows, own_cols = own_shapes[a][1:]
        if a < 2:
            row = row + owner * own_rows
        else:
            col = col + owner * own_cols
        return (layer, pl.ds(pl.multiple_of(row, 16), rows), pl.ds(pl.multiple_of(col, 128), width))

    def own_slice(a, layer, row, rows, col):
        return (layer, pl.ds(pl.multiple_of(row, 16), rows), pl.ds(pl.multiple_of(col, 128), width))

    def remote(src, dst, send, recv, rank):
        return pltpu.make_async_remote_copy(
            src_ref=src, dst_ref=dst, send_sem=send, recv_sem=recv,
            device_id={"rep": rank}, device_id_type=MESH,
        )

    def wait_bytes(ref, sem):
        pltpu.make_async_copy(ref, ref, sem).wait()

    def fetch(k):
        for i in range(m):
            j = jnp.where(first, m - 1 - i, i)
            for a, layer, row, rows, col, at in blocks(k):
                there = pl.ds(at, rows)
                remote(
                    deltas[a].at[(0,) + whole_slice(a, layer, row, rows, col, 2 * j + 1 - core)],
                    theirs.at[k, j, there], total_sem.at[0], theirs_sem.at[k, j], partner,
                ).start()
                pltpu.make_async_copy(
                    deltas[a].at[(0,) + whole_slice(a, layer, row, rows, col, 2 * j + core)],
                    mine.at[k, j, there], mine_sem.at[k, j],
                ).start()
        for a, layer, row, rows, col, at in blocks(k):
            there, own = pl.ds(at, rows), own_slice(a, layer, row, rows, col)
            pltpu.make_async_copy(masters[a].at[own], master.at[k, there], state_sem.at[k]).start()
            pltpu.make_async_copy(moments[a].at[own], moment.at[k, there], state_sem.at[k]).start()

    def pair_sum(k, j):
        wait_bytes(theirs.at[k, j], theirs_sem.at[k, j])
        wait_bytes(mine.at[k, j], mine_sem.at[k, j])
        return theirs[k, j].astype(jnp.float32) + mine[k, j].astype(jnp.float32)

    def send_up(k, j):
        remote(mine.at[k, j], up_in.at[k, j], total_sem.at[1], up_sem.at[k, j], above).start()

    def send_down(k, j):
        remote(mine.at[k, j], down_in.at[k, j], total_sem.at[1], down_sem.at[k, j], below).start()

    def begin(k):
        @pl.when(first | last)
        def _():
            for i in range(m - 1):
                j = jnp.where(first, m - 1 - i, i)
                mine[k, j] = pair_sum(k, j).astype(jnp.bfloat16)

                @pl.when(first)
                def _():
                    send_up(k, j)

                @pl.when(last)
                def _():
                    send_down(k, j)

    def forward(s, k):
        up_j = m - 1 + z - s

        @pl.when((z >= 1) & (z <= s) & (z < m - 1))
        def _():
            running = pair_sum(k, up_j)
            wait_bytes(up_in.at[k, up_j], up_sem.at[k, up_j])
            mine[k, up_j] = (running + up_in[k, up_j].astype(jnp.float32)).astype(jnp.bfloat16)
            send_up(k, up_j)

        down_j = s - (m - 1 - z)

        @pl.when((z < m - 1) & (m - 1 - z <= s) & (z >= 1))
        def _():
            running = pair_sum(k, down_j)
            wait_bytes(down_in.at[k, down_j], down_sem.at[k, down_j])
            mine[k, down_j] = (running + down_in[k, down_j].astype(jnp.float32)).astype(jnp.bfloat16)
            send_down(k, down_j)

    def hand_on(k, j, up, down):
        chunk = gathered.at[k, j]

        @pl.when(up)
        def _():
            remote(chunk, chunk, gather_up_sem.at[k, j], gather_sem.at[k, j], above).start()

        @pl.when(down)
        def _():
            remote(chunk, chunk, gather_down_sem.at[k, j], gather_sem.at[k, j], below).start()

        for a, layer, row, rows, col, at in blocks(k):
            source = gathered.at[k, j, pl.ds(at, rows)]
            target = params[a].at[whole_slice(a, layer, row, rows, col, 2 * j + core)]
            remote(source, target, total_sem.at[2], total_sem.at[3], partner).start()
            pltpu.make_async_copy(source, target, total_sem.at[4]).start()

    def update(k):
        total = pair_sum(k, z)
        pltpu.make_async_copy(master.at[k], master.at[k], state_sem.at[k]).wait()
        pltpu.make_async_copy(moment.at[k], moment.at[k], state_sem.at[k]).wait()
        mine_total = total

        def finish(summed):
            average = summed / n
            momentum = OUTER_MOMENTUM * moment[k] + average
            updated = master[k] - OUTER_RATE * (average + OUTER_MOMENTUM * momentum)
            moment[k] = momentum
            master[k] = updated
            gathered[k, z] = updated.astype(jnp.bfloat16)

        @pl.when(z > 0)
        def _():
            wait_bytes(up_in.at[k, z], up_sem.at[k, z])

        @pl.when(z < m - 1)
        def _():
            wait_bytes(down_in.at[k, z], down_sem.at[k, z])

        @pl.when(first)
        def _():
            finish(mine_total + down_in[k, z].astype(jnp.float32))

        @pl.when(last)
        def _():
            finish(mine_total + up_in[k, z].astype(jnp.float32))

        @pl.when(jnp.logical_not(first | last))
        def _():
            finish(mine_total + up_in[k, z].astype(jnp.float32) + down_in[k, z].astype(jnp.float32))

        hand_on(k, z, z < m - 1, z > 0)
        for a, layer, row, rows, col, at in blocks(k):
            there, own = pl.ds(at, rows), own_slice(a, layer, row, rows, col)
            pltpu.make_async_copy(master.at[k, there], new_masters[a].at[own], total_sem.at[5]).start()
            pltpu.make_async_copy(moment.at[k, there], new_moments[a].at[own], total_sem.at[6]).start()

    def gather(g, k):
        low, high = z - g, z + g

        @pl.when(low >= 0)
        def _():
            wait_bytes(gathered.at[k, low], gather_sem.at[k, low])
            hand_on(k, low, z < m - 1, False)

        @pl.when(high < m)
        def _():
            wait_bytes(gathered.at[k, high], gather_sem.at[k, high])
            hand_on(k, high, False, z > 0)

    barrier = pltpu.get_barrier_semaphore()
    pl.semaphore_signal(barrier, inc=1, device_id={"rep": partner}, device_id_type=MESH)

    @pl.when(z > 0)
    def _():
        pl.semaphore_signal(barrier, inc=1, device_id={"rep": below}, device_id_type=MESH)

    @pl.when(z < m - 1)
    def _():
        pl.semaphore_signal(barrier, inc=1, device_id={"rep": above}, device_id_type=MESH)

    pl.semaphore_wait(barrier, 1 + (z > 0).astype(jnp.int32) + (z < m - 1).astype(jnp.int32))

    stages = [begin]
    stages += [functools.partial(forward, s) for s in range(1, m - 1)]
    stages += [update]
    stages += [functools.partial(gather, g) for g in range(1, m)]
    lead = min(LEAD, pieces)

    def early(k, carry):
        fetch(k)
        return carry

    lax.fori_loop(0, lead, early, 0)

    def tick(t, carry):
        @pl.when(t + lead < pieces)
        def _():
            fetch(t + lead)

        for s in reversed(range(len(stages))):
            k = t - s

            @pl.when((k >= 0) & (k < pieces))
            def _():
                stages[s](k)

        return carry

    lax.fori_loop(0, pieces + len(stages) - 1, tick, 0)

    wait_bytes(theirs, total_sem.at[0])
    wait_bytes(theirs.at[:, pl.ds(0, m - 1)], total_sem.at[1])
    for s in range(2, 5):
        wait_bytes(gathered, total_sem.at[s])
    wait_bytes(master, total_sem.at[5])
    wait_bytes(moment, total_sem.at[6])

    def drain(k, carry):
        for j in range(m):
            @pl.when((z < m - 1) & (j <= z))
            def _():
                wait_bytes(gathered.at[k, j], gather_up_sem.at[k, j])

            @pl.when((z > 0) & (j >= z))
            def _():
                wait_bytes(gathered.at[k, j], gather_down_sem.at[k, j])
        return carry

    lax.fori_loop(0, pieces, drain, 0)


def on_device(n, *arrays):
    states = arrays[1::3]
    own_shapes = [x.shape for x in states]
    pieces = PIECES
    while plan(own_shapes, pieces) is None:
        pieces //= 2
    cuts = plan(own_shapes, pieces)
    width = min(cols for _, _, _, cols in cuts)
    while any(cols % width for _, _, _, cols in cuts):
        width -= 128
    depth = sum(rows * (cols // width) for _, _, rows, cols in cuts)
    m = n // 2
    out_shape = []
    for delta, master, moment in zip(arrays[0::3], arrays[1::3], arrays[2::3]):
        out_shape += [
            jax.ShapeDtypeStruct(delta.shape[1:], jnp.bfloat16),
            jax.ShapeDtypeStruct(master.shape, jnp.float32),
            jax.ShapeDtypeStruct(moment.shape, jnp.float32),
        ]
    chunks = pltpu.VMEM((pieces, m, depth, width), jnp.bfloat16)
    state = pltpu.VMEM((pieces, depth, width), jnp.float32)
    flags = pltpu.SemaphoreType.DMA((pieces, m))
    return tuple(
        pl.pallas_call(
            functools.partial(kernel, n, cuts, width, own_shapes),
            out_shape=out_shape,
            in_specs=[pl.BlockSpec(memory_space=pl.ANY)] * len(arrays),
            out_specs=[pl.BlockSpec(memory_space=pl.ANY)] * len(out_shape),
            scratch_shapes=[chunks] * 5 + [state] * 2
            + [flags] * 5 + [pltpu.SemaphoreType.DMA((pieces,))] + [flags] * 2
            + [pltpu.SemaphoreType.DMA((7,))],
            compiler_params=pltpu.CompilerParams(
                collective_id=0, has_side_effects=True, vmem_limit_bytes=60 * 1024 * 1024
            ),
        )(*arrays)
    )


def solution(mesh):
    placed = (
        P("rep", None, None, "tp"),
        P(None, "rep", "tp"),
        P(None, "rep", "tp"),
        P("rep", None, None, "tp"),
        P(None, "rep", "tp"),
        P(None, "rep", "tp"),
        P("rep", None, "tp", None),
        P(None, "tp", "rep"),
        P(None, "tp", "rep"),
    )
    return jax.shard_map(
        functools.partial(on_device, mesh.shape["rep"]),
        mesh=mesh,
        in_specs=placed,
        out_specs=(
            P(None, None, "tp"),
            P(None, "rep", "tp"),
            P(None, "rep", "tp"),
            P(None, None, "tp"),
            P(None, "rep", "tp"),
            P(None, "rep", "tp"),
            P(None, "tp", None),
            P(None, "tp", "rep"),
            P(None, "tp", "rep"),
        ),
        check_vma=False,
    )
```

time: 332 us -> 183 us (0.55)
  waiting for transfers between devices: 298 us -> 0 us
  Pallas kernels: 0 us -> 164 us
  between operations: 14.1 us -> 0.67 us
  other arithmetic: 9.27 us -> 0 us
  local copies, waits for them, and re-layouts: 11 us -> 18.2 us
    pallas_call x0 -> x1, Pallas kernels: none -> 164 us  [on_device(): pl.pallas_call(functools.partial(kernel, n, cuts, width, own_shapes), out...]
    reduce_scatter x3 -> x0, waiting for transfers between devices: 155 us -> none  [the longest x1 66.8 us: outer_step(): lax.psum_scatter(delta_query[0].astype(jnp.float32).astype(jnp.bfloat16),...]
    all_gather x3 -> x0, waiting for transfers between devices: 140 us -> none  [the longest x1 64.9 us: outer_step(): lax.all_gather(query_master.astype(jnp.bfloat16), 'rep', axis=1, tiled=True)]
    convert_element_type x3 -> x0, other arithmetic: 9.27 us -> none  [the longest x1 3.63 us: outer_step(): output_master.astype(jnp.bfloat16)]
    unnamed x15 -> x25, local copies, waits for them, and re-layouts: 11 us -> 18.2 us
  transfers between devices with their start and end apart: 6 -> 0, of which waited for: 6 -> 0; matrix products, arithmetic and copies ran while one was open for 3% -> 0% of each run, Pallas kernels for 0% -> 0%
where the time goes in v1:
time: 183 us
  Pallas kernels  164 us (90%)
  local copies, waits for them, and re-layouts  18.2 us (10%)
    pallas_call x1, Pallas kernels, on_device(): pl.pallas_call(functools.partial(kernel, n, cuts, width, own_shapes), out...  164 us
    unnamed x25, local copies, waits for them, and re-layouts  18.2 us

profile of v1, /device:TPU:0, one launch (start us, length us, event | category | flops | bytes accessed | tf_op | source)
XLA Modules:
  0.0 183.0 jit_solution(16027890545843431828)
XLA Ops:
  0.6 164.0 %shard_map.160 = (bf16[2,2048,768]{2,1,0:T(8,128)(2,1)}, f32[2,256,768]{2,1,0:T(8,128)}, f32[2,256,768]{2,1,0:T(8,128)}, bf16[2,512,1024]{2,1,0:T(8,128)(2,1)}, ...) custom-call(bf16[1,2,2048,768]{3,2,1,0:T(8,128)(2,1)} %refs_0_.1, ...), custom_call_target="tpu_custom_call" | custom-call | tf_op jit(solution)/shard_map/pallas_call | solution.py:295
  164.7 0.0 copy-start.3
  164.7 6.0 %copy.27 = bf16[2,2048,768]{2,1,0:T(8,128)(2,1)} copy(bf16[2,2048,768]{2,1,0:T(8,128)(2,1)} %get-tuple-element.18) | data formatting | bytes 12582912
  170.7 0.0 copy-done.3
  170.7 0.0 copy-start.2
  170.7 1.1 copy.28
  171.9 0.8 copy-done.2
  172.7 0.0 copy-start.1
  172.7 0.0 copy-start.7
  172.7 1.1 copy.29
  173.8 1.0 copy-done.1
  174.9 0.0 copy-start.6
  174.9 0.0 copy-start
  174.9 1.3 copy.30
  176.2 0.0 copy-done.7
  176.2 0.8 copy.31
  177.0 0.0 copy-done.6
  177.0 0.8 copy.32
  177.8 0.6 copy-done
  178.4 0.0 copy-start.5
  178.4 2.0 %copy.33 = bf16[2,512,2048]{2,1,0:T(8,128)(2,1)} copy(bf16[2,512,2048]{2,1,0:T(8,128)(2,1)S(1)} %copy-done) | data formatting | bytes 8388608
  180.4 0.0 copy-done.5
  180.4 0.0 copy-start.4
  180.4 1.0 copy.34
  181.4 0.6 copy-done.4
  182.0 1.0 copy.35
Async XLA Ops:
  164.7 6.0 %copy-start.3 = (f32[2,256,768]{2,1,0:T(8,128)S(1)}, f32[2,256,768]{2,1,0:T(8,128)}, u32[]{:S(2)}) copy-start(f32[2,256,768]{2,1,0:T(8,128)} %get-tuple-element.19) | copy-start | bytes 4718596
  170.7 2.0 %copy-start.2 = (f32[2,256,768]{2,1,0:T(8,128)S(1)}, f32[2,256,768]{2,1,0:T(8,128)}, u32[]{:S(2)}) copy-start(f32[2,256,768]{2,1,0:T(8,128)} %get-tuple-element.20) | copy-start | bytes 4718596
  172.7 2.2 %copy-start.1 = (bf16[2,512,1024]{2,1,0:T(8,128)(2,1)S(1)}, bf16[2,512,1024]{2,1,0:T(8,128)(2,1)}, u32[]{:S(2)}) copy-start(bf16[2,512,1024]{2,1,0:T(8,128)(2,1)} %get-tuple-element.21) | copy-start | bytes 6291460
  172.7 3.5 %copy-start.7 = (f32[2,64,1024]{2,1,0:T(8,128)S(1)}, f32[2,64,1024]{2,1,0:T(8,128)}, u32[]{:S(2)}) copy-start(f32[2,64,1024]{2,1,0:T(8,128)} %get-tuple-element.22) | copy-start | bytes 1572868
  174.9 2.1 %copy-start.6 = (f32[2,64,1024]{2,1,0:T(8,128)S(1)}, f32[2,64,1024]{2,1,0:T(8,128)}, u32[]{:S(2)}) copy-start(f32[2,64,1024]{2,1,0:T(8,128)} %get-tuple-element.23) | copy-start | bytes 1572868
  174.9 3.5 %copy-start = (bf16[2,512,2048]{2,1,0:T(8,128)(2,1)S(1)}, bf16[2,512,2048]{2,1,0:T(8,128)(2,1)}, u32[]{:S(2)}) copy-start(bf16[2,512,2048]{2,1,0:T(8,128)(2,1)} %get-tuple-element.24) | copy-start | bytes 12582916
  178.4 2.0 %copy-start.5 = (f32[2,512,256]{2,1,0:T(8,128)S(1)}, f32[2,512,256]{2,1,0:T(8,128)}, u32[]{:S(2)}) copy-start(f32[2,512,256]{2,1,0:T(8,128)} %get-tuple-element.25) | copy-start | bytes 3145732
  180.4 1.6 copy-start.4

commit v2 on v1

v2 whole, which is shorter than its diff:
```python
import functools

import jax
import jax.numpy as jnp
from jax import lax
from jax.experimental import pallas as pl
from jax.experimental.pallas import tpu as pltpu
from jax.sharding import PartitionSpec as P

OUTER_RATE = 0.7
OUTER_MOMENTUM = 0.9
MESH = pl.DeviceIdType.MESH
PIECES = 16
LEAD = 3


def plan(shapes, pieces):
    cuts = []
    for layers, rows, cols in shapes:
        if pieces % layers:
            return None
        per_layer = pieces // layers
        by_row = per_layer
        while by_row > 1 and (rows % by_row or (rows // by_row) % 16):
            by_row //= 2
        by_col = per_layer // by_row
        if by_row * by_col != per_layer or cols % by_col or (cols // by_col) % 128:
            return None
        cuts.append((per_layer, by_col, rows // by_row, cols // by_col))
    return cuts


def kernel(n, cuts, own_shapes, *refs):
    deltas, masters, moments = refs[0:9:3], refs[1:9:3], refs[2:9:3]
    params, new_masters, new_moments = refs[9:18:3], refs[10:18:3], refs[11:18:3]
    theirs, mine, up_in, down_in = refs[18:21], refs[21:24], refs[24:27], refs[27:30]
    (measure, theirs_sem, mine_sem, up_sem, down_sem, gather_sem,
     gather_up_sem, gather_down_sem, total_sem) = refs[30:]
    m = n // 2
    pieces = theirs[0].shape[0]
    me = lax.axis_index("rep")
    z, core = me // 2, me % 2
    partner = z * 2 + 1 - core
    above, below = (z + 1) * 2 + core, (z - 1) * 2 + core
    first, last = z == 0, z == m - 1
    arrays = range(len(cuts))

    def own_slice(a, k):
        per_layer, by_col, rows, cols = cuts[a]
        layer, part = k // per_layer, k % per_layer
        if by_col == 1:
            return (layer, pl.ds(pl.multiple_of(part * rows, 16), rows), pl.ds(0, cols))
        row, col = (part // by_col) * rows, (part % by_col) * cols
        return (layer, pl.ds(pl.multiple_of(row, 16), rows), pl.ds(pl.multiple_of(col, 128), cols))

    def whole_slice(a, k, owner):
        per_layer, by_col, rows, cols = cuts[a]
        layer, part = k // per_layer, k % per_layer
        row, col = (part // by_col) * rows, (part % by_col) * cols
        own_rows, own_cols = own_shapes[a][1:]
        if a < 2:
            row = row + owner * own_rows
        else:
            col = col + owner * own_cols
        if a < 2 and by_col == 1:
            return (layer, pl.ds(pl.multiple_of(row, 16), rows), pl.ds(0, cols))
        return (layer, pl.ds(pl.multiple_of(row, 16), rows), pl.ds(pl.multiple_of(col, 128), cols))

    def remote(src, dst, send, recv, rank):
        return pltpu.make_async_remote_copy(
            src_ref=src, dst_ref=dst, send_sem=send, recv_sem=recv,
            device_id={"rep": rank}, device_id_type=MESH,
        )

    def wait_bytes(ref, sem):
        pltpu.make_async_copy(ref, ref, sem).wait()

    def wait_chunk(sem):
        wait_bytes(measure, sem)

    def fetch(k):
        for i in range(m):
            j = jnp.where(first, m - 1 - i, i)
            for a in arrays:
                remote(
                    deltas[a].at[(0,) + whole_slice(a, k, 2 * j + 1 - core)],
                    theirs[a].at[k, j], total_sem.at[0, a], theirs_sem.at[k, j], partner,
                ).start()
                pltpu.make_async_copy(
                    deltas[a].at[(0,) + whole_slice(a, k, 2 * j + core)],
                    mine[a].at[k, j], mine_sem.at[k, j],
                ).start()

    def wait_pair(k, j):
        wait_chunk(theirs_sem.at[k, j])
        wait_chunk(mine_sem.at[k, j])

    def pair_sum(a, k, j):
        return theirs[a][k, j].astype(jnp.float32) + mine[a][k, j].astype(jnp.float32)

    def send_up(k, j):
        for a in arrays:
            remote(mine[a].at[k, j], up_in[a].at[k, j], total_sem.at[1, a], up_sem.at[k, j], above).start()

    def send_down(k, j):
        for a in arrays:
            remote(mine[a].at[k, j], down_in[a].at[k, j], total_sem.at[1, a], down_sem.at[k, j], below).start()

    def begin(k):
        @pl.when(first | last)
        def _():
            for i in range(m - 1):
                j = jnp.where(first, m - 1 - i, i)
                wait_pair(k, j)
                for a in arrays:
                    mine[a][k, j] = pair_sum(a, k, j).astype(jnp.bfloat16)

                @pl.when(first)
                def _():
                    send_up(k, j)

                @pl.when(last)
                def _():
                    send_down(k, j)

    def forward(s, k):
        up_j = m - 1 + z - s

        @pl.when((z >= 1) & (z <= s) & (z < m - 1))
        def _():
            wait_pair(k, up_j)
            wait_chunk(up_sem.at[k, up_j])
            for a in arrays:
                running = pair_sum(a, k, up_j) + up_in[a][k, up_j].astype(jnp.float32)
                mine[a][k, up_j] = running.astype(jnp.bfloat16)
            send_up(k, up_j)

        down_j = s - (m - 1 - z)

        @pl.when((z < m - 1) & (m - 1 - z <= s) & (z >= 1))
        def _():
            wait_pair(k, down_j)
            wait_chunk(down_sem.at[k, down_j])
            for a in arrays:
                running = pair_sum(a, k, down_j) + down_in[a][k, down_j].astype(jnp.float32)
                mine[a][k, down_j] = running.astype(jnp.bfloat16)
            send_down(k, down_j)

    def hand_on(k, j, up, down):
        chunks = [params[a].at[whole_slice(a, k, 2 * j + core)] for a in arrays]

        @pl.when(up)
        def _():
            for chunk in chunks:
                remote(chunk, chunk, gather_up_sem.at[k, j], gather_sem.at[k, j], above).start()

        @pl.when(down)
        def _():
            for chunk in chunks:
                remote(chunk, chunk, gather_down_sem.at[k, j], gather_sem.at[k, j], below).start()

        for a in arrays:
            remote(chunks[a], chunks[a], total_sem.at[2, a], total_sem.at[3, a], partner).start()

    def update(k):
        wait_pair(k, z)

        @pl.when(k == 0)
        def _():
            for a in arrays:
                wait_bytes(new_masters[a], total_sem.at[4, a])
                wait_bytes(new_moments[a], total_sem.at[5, a])

        @pl.when(z > 0)
        def _():
            wait_chunk(up_sem.at[k, z])

        @pl.when(z < m - 1)
        def _():
            wait_chunk(down_sem.at[k, z])

        def finish(neighbours):
            for a in arrays:
                summed = pair_sum(a, k, z)
                for near in neighbours:
                    summed = summed + near[a][k, z].astype(jnp.float32)
                own = own_slice(a, k)
                average = summed / n
                momentum = OUTER_MOMENTUM * new_moments[a][own] + average
                updated = new_masters[a][own] - OUTER_RATE * (average + OUTER_MOMENTUM * momentum)
                new_moments[a][own] = momentum
                new_masters[a][own] = updated
                params[a][whole_slice(a, k, me)] = updated.astype(jnp.bfloat16)

        @pl.when(first)
        def _():
            finish((down_in,))

        @pl.when(last)
        def _():
            finish((up_in,))

        @pl.when(jnp.logical_not(first | last))
        def _():
            finish((up_in, down_in))

        hand_on(k, z, z < m - 1, z > 0)

    def gather(g, k):
        low, high = z - g, z + g

        @pl.when(low >= 0)
        def _():
            wait_chunk(gather_sem.at[k, low])
            hand_on(k, low, z < m - 1, False)

        @pl.when(high < m)
        def _():
            wait_chunk(gather_sem.at[k, high])
            hand_on(k, high, False, z > 0)

    barrier = pltpu.get_barrier_semaphore()
    pl.semaphore_signal(barrier, inc=1, device_id={"rep": partner}, device_id_type=MESH)

    @pl.when(z > 0)
    def _():
        pl.semaphore_signal(barrier, inc=1, device_id={"rep": below}, device_id_type=MESH)

    @pl.when(z < m - 1)
    def _():
        pl.semaphore_signal(barrier, inc=1, device_id={"rep": above}, device_id_type=MESH)

    pl.semaphore_wait(barrier, 1 + (z > 0).astype(jnp.int32) + (z < m - 1).astype(jnp.int32))

    stages = [begin]
    stages += [functools.partial(forward, s) for s in range(1, m - 1)]
    stages += [update]
    stages += [functools.partial(gather, g) for g in range(1, m)]
    lead = min(LEAD, pieces)

    def early(k, carry):
        fetch(k)
        return carry

    lax.fori_loop(0, lead, early, 0)
    for a in arrays:
        pltpu.make_async_copy(masters[a], new_masters[a], total_sem.at[4, a]).start()
        pltpu.make_async_copy(moments[a], new_moments[a], total_sem.at[5, a]).start()

    def tick(t, carry):
        @pl.when(t + lead < pieces)
        def _():
            fetch(t + lead)

        for s in reversed(range(len(stages))):
            k = t - s

            @pl.when((k >= 0) & (k < pieces))
            def _():
                stages[s](k)

        return carry

    lax.fori_loop(0, pieces + len(stages) - 1, tick, 0)

    for a in arrays:
        wait_bytes(theirs[a], total_sem.at[0, a])
        wait_bytes(theirs[a].at[:, pl.ds(0, m - 1)], total_sem.at[1, a])
        wait_bytes(theirs[a], total_sem.at[2, a])
        wait_bytes(theirs[a], total_sem.at[3, a])

    def drain(k, carry):
        for j in range(m):
            @pl.when((z < m - 1) & (j <= z))
            def _():
                wait_chunk(gather_up_sem.at[k, j])

            @pl.when((z > 0) & (j >= z))
            def _():
                wait_chunk(gather_down_sem.at[k, j])
        return carry

    lax.fori_loop(0, pieces, drain, 0)


def on_device(n, *arrays):
    states = arrays[1::3]
    own_shapes = [x.shape for x in states]
    pieces = PIECES
    while plan(own_shapes, pieces) is None:
        pieces //= 2
    cuts = plan(own_shapes, pieces)
    m = n // 2
    size = sum(rows * cols for _, _, rows, cols in cuts)
    out_shape = []
    for delta, master, moment in zip(arrays[0::3], arrays[1::3], arrays[2::3]):
        out_shape += [
            pltpu.VMEM(delta.shape[1:], jnp.bfloat16),
            pltpu.VMEM(master.shape, jnp.float32),
            pltpu.VMEM(moment.shape, jnp.float32),
        ]
    chunks = [pltpu.VMEM((pieces, m, rows, cols), jnp.bfloat16) for _, _, rows, cols in cuts]
    flags = pltpu.SemaphoreType.DMA((pieces, m))
    scratch_bytes = 4 * 2 * pieces * m * size
    return tuple(
        pl.pallas_call(
            functools.partial(kernel, n, cuts, own_shapes),
            out_shape=out_shape,
            in_specs=[pl.BlockSpec(memory_space=pltpu.HBM)] * len(arrays),
            out_specs=[pl.BlockSpec(memory_space=pltpu.VMEM)] * len(out_shape),
            scratch_shapes=chunks * 4
            + [pltpu.VMEM((size // 128, 128), jnp.bfloat16)]
            + [flags] * 7
            + [pltpu.SemaphoreType.DMA((6, len(cuts)))],
            compiler_params=pltpu.CompilerParams(
                collective_id=0, has_side_effects=True, vmem_limit_bytes=scratch_bytes + 4 * 2**20
            ),
        )(*arrays)
    )


def solution(mesh):
    placed = (
        P("rep", None, None, "tp"),
        P(None, "rep", "tp"),
        P(None, "rep", "tp"),
        P("rep", None, None, "tp"),
        P(None, "rep", "tp"),
        P(None, "rep", "tp"),
        P("rep", None, "tp", None),
        P(None, "tp", "rep"),
        P(None, "tp", "rep"),
    )
    return jax.shard_map(
        functools.partial(on_device, mesh.shape["rep"]),
        mesh=mesh,
        in_specs=placed,
        out_specs=(
            P(None, None, "tp"),
            P(None, "rep", "tp"),
            P(None, "rep", "tp"),
            P(None, None, "tp"),
            P(None, "rep", "tp"),
            P(None, "rep", "tp"),
            P(None, "tp", None),
            P(None, "tp", "rep"),
            P(None, "tp", "rep"),
        ),
        check_vma=False,
    )
```

time: 183 us -> 184 us (level)
    unnamed x25 -> x21, local copies, waits for them, and re-layouts: 18.2 us -> 19.2 us
where the time goes in v2:
time: 184 us
  Pallas kernels  164 us (89%)
  local copies, waits for them, and re-layouts  19.2 us (10%)
    pallas_call x1, Pallas kernels, on_device(): pl.pallas_call(functools.partial(kernel, n, cuts, own_shapes), out_shape=...  164 us
    unnamed x21, local copies, waits for them, and re-layouts  19.2 us

profile of v2, /device:TPU:0, one launch (start us, length us, event | category | flops | bytes accessed | tf_op | source)
XLA Modules:
  0.0 183.8 jit_solution(6777957924412011939)
XLA Ops:
  0.6 0.0 copy-start
  0.7 1.4 copy-done
  2.1 0.0 copy-start.1
  2.1 1.4 copy-done.1
  3.5 0.0 copy-start.2
  3.5 1.2 copy-done.2
  4.7 0.0 copy-start.3
  4.7 1.2 copy-done.3
  5.9 0.0 copy-start.4
  5.9 1.0 copy-done.4
  7.0 0.0 copy-start.5
  7.0 1.0 copy-done.5
  8.0 164.0 %shard_map.160 = (bf16[2,2048,768]{2,1,0:T(8,128)(2,1)S(1)}, f32[2,256,768]{2,1,0:T(8,128)S(1)}, f32[2,256,768]{2,1,0:T(8,128)S(1)}, bf16[2,512,1024]{2,1,0:T(8,...) custom-call(bf16[1,2,2048,768]{3,2,1,0:T(8,128)(2,1)} %refs_0_.1, ...), custom_call_target="tpu_custom_call" | custom-call | tf_op jit(solution)/shard_map/pallas_call | solution.py:306
  172.0 2.7 %copy.27 = bf16[2,2048,768]{2,1,0:T(8,128)(2,1)} copy(bf16[2,2048,768]{2,1,0:T(8,128)(2,1)S(1)} %get-tuple-element.9) | data formatting | bytes 12582912
  174.7 0.8 copy.31
  175.5 0.8 copy.32
  176.3 1.0 copy.34
  177.3 1.0 copy.35
  178.2 1.1 copy.28
  179.4 1.1 copy.29
  180.5 1.3 copy.30
  181.8 2.0 %copy.33 = bf16[2,512,2048]{2,1,0:T(8,128)(2,1)} copy(bf16[2,512,2048]{2,1,0:T(8,128)(2,1)S(1)} %get-tuple-element.15) | data formatting | bytes 8388608
Async XLA Ops:
  0.6 1.4 copy-start
  2.1 1.4 copy-start.1
  3.5 1.2 copy-start.2
  4.7 1.2 copy-start.3
  5.9 1.0 copy-start.4
  7.0 1.0 copy-start.5
